TPU v7x, 256 devices: a whole 4x4x8 slice. The times are simulated.
256 devices in a mesh: band: 8 (over y_lo, x), ga: 32 (over z, y_hi, core).
Axes of the slice: x: 4, y: 4 (y_hi: 2, y_lo: 2; y = y_hi * 2 + y_lo), z: 8, core: 2. Of those that a mesh axis runs over, the one named last changes fastest.
Arguments:
- wavefunctions: bfloat16 [1024, 98304], P('band', 'ga'), may hold values from -6 to 6
- projectors: bfloat16 [2048, 98304], P('band', 'ga'), may hold values from -0.125 to 0.125
- kinetic_diag: float32 [98304], P('ga'), may hold values from 0.1 to 4
- species_index: int32 [256], replicated, may hold values from 0 to 3
- coupling: float32 [4, 8, 8], replicated, may hold values from -5 to 5
Outputs:
- applied: bfloat16 [1024, 98304], P('band', 'ga')
All inputs are finite; a program needn't handle non-finite values.
Results may differ from a plain program's by a relative error of at most 0.015.
Values may be sent and summed in bfloat16 or wider, within the bound.
A program may use at most 64 MiB of HBM per device.

v0:
```python
import jax
import jax.numpy as jnp
from jax import lax
from jax.sharding import PartitionSpec as P

NPA = 8


def in_blocks(array, dim, length):
    dims = array.shape
    blocks = array.reshape(*dims[:dim], length, dims[dim] // length, *dims[dim + 1 :])
    return jnp.moveaxis(blocks, dim, 0)


def summed_on_arrival(array, axis, dim):
    length = lax.axis_size(axis)
    blocks = lax.all_to_all(in_blocks(array, dim, length), axis, 0, 0, tiled=True)
    return jnp.sum(blocks.astype(jnp.float32), axis=0)


def laid_out(blocks, dim):
    blocks = jnp.moveaxis(blocks, 0, dim)
    dims = blocks.shape
    return blocks.reshape(*dims[:dim], dims[dim] * dims[dim + 1], *dims[dim + 2 :])


def sent_to_all(array, axis):
    copies = jnp.broadcast_to(array, (lax.axis_size(axis), *array.shape))
    return lax.all_to_all(copies, axis, split_axis=0, concat_axis=0, tiled=True)


def collect(array, axis, dim):
    return laid_out(sent_to_all(array, axis), dim)


def apply_blocks(correlations, species_index, coupling, atom_start):
    rows = correlations.shape[0]
    count = correlations.shape[1] // NPA
    local_species = lax.dynamic_slice_in_dim(species_index, atom_start, count)
    onehot = (
        local_species[:, None] == jnp.arange(coupling.shape[0], dtype=jnp.int32)[None, :]
    ).astype(jnp.float32)
    blocks = jnp.einsum("as,sij->aij", onehot, coupling)
    mixed = jnp.einsum("baj,aij->bai", correlations.reshape(rows, count, NPA), blocks)
    return mixed.reshape(rows, count * NPA).astype(jnp.bfloat16)


def reduce_and_mix(partial_value, species_index, coupling):
    share = summed_on_arrival(partial_value.astype(jnp.bfloat16), "ga", 1)
    width = share.shape[1]
    start = lax.axis_index("ga") * width // NPA
    mixed = apply_blocks(share, species_index, coupling, start)
    return collect(mixed, "ga", 1)


def local(wavefunctions, projectors, kinetic_diag, species_index, coupling):
    all_proj = lax.all_gather(projectors, "band", axis=0, tiled=True)
    partial_value = jnp.einsum(
        "bg,pg->bp", wavefunctions, all_proj, preferred_element_type=jnp.float32
    )
    mixed = reduce_and_mix(partial_value, species_index, coupling)
    nonlocal_term = jnp.dot(mixed, all_proj, preferred_element_type=jnp.float32)
    return (kinetic_diag[None, :] * wavefunctions.astype(jnp.float32) + nonlocal_term).astype(
        jnp.bfloat16
    )


def solution(mesh):
    in_specs = (P("band", "ga"), P("band", "ga"), P("ga"), P(), P())
    out_specs = P("band", "ga")
    return jax.shard_map(local, mesh=mesh, in_specs=in_specs, out_specs=out_specs, check_vma=False)
```

profile of v0, /device:TPU:1, one launch (start us, length us, event | category | flops | bytes accessed | tf_op | source)
XLA Modules:
  0.0 220.6 jit_solution(2043861242640377641)
XLA Ops:
  6.5 0.0 copy-start
  6.5 0.0 copy-start.1
  6.5 0.0 copy-start.3
  6.5 0.0 copy-start.2
  6.5 0.0 all-gather.2.cloned.1.call-start
  6.6 0.7 all-gather.2.cloned.1.call-update
  7.3 139.2 %all-gather.2.cloned.1.call-done = bf16[2048,3072]{1,0:T(8,128)(2,1)} async-done(((bf16[256,3072]{1,0:T(8,128)(2,1)}), bf16[2048,3072]{1,0:T(8,128)(2,1)}) %all-gather.2.cloned.1.call-update) | async-done | bytes 12582928 | tf_op jit(solution)/shard_map/all_gather | solution.py:57
  146.5 9.1 %convolution_convert_fusion = bf16[128,2048]{1,0:T(8,128)(2,1)S(1)} fusion(bf16[128,3072]{1,0:T(8,128)(2,1)} %param.5, bf16[2048,3072]{1,0:T(8,128)(2,1)} %all-gather.2.cloned.1.call-done), kind=kOutput, calls=%fused_computation.2 | convolution fusion | flops 1610874880 | bytes 13893632 | tf_op jit(solution)/shard_map/bg,pg->bp/dot_general | solution.py:58
  155.6 1.0 copy.7
  156.6 10.2 %all-to-all-start = ((bf16[32,128,64]{1,2,0:T(8,128)(2,1)}), bf16[32,128,64]{1,2,0:T(8,128)(2,1)S(1)}, u32[]{:S(2)}, u32[]{:S(2)}) async-start(bf16[32,128,64]{1,2,0:T(8,128)(2,1)} %bitcast.2), calls=%async_computation | async-start | bytes 1048576 | tf_op jit(solution)/shard_map/all_to_all | solution.py:17
  166.8 0.0 copy-done.3
  166.8 0.1 dynamic_slice.3
  166.9 0.0 copy-done
  166.9 0.2 fusion.4
  167.1 16.6 %all-to-all-done = bf16[32,128,64]{1,2,0:T(8,128)(2,1)S(1)} async-done(((bf16[32,128,64]{1,2,0:T(8,128)(2,1)}), bf16[32,128,64]{1,2,0:T(8,128)(2,1)S(1)}, u32[]{:S(2)}, u32[]{:S(2)}) %all-to-all-start) | async-done | bytes 524320 | tf_op jit(solution)/shard_map/all_to_all | solution.py:17
  183.6 0.1 convert_reduce_fusion
  183.7 0.1 fusion.1
  183.8 0.1 broadcast_in_dim.2
  183.9 22.5 %all_to_all.10 = bf16[32,128,64]{1,2,0:T(8,128)(2,1)S(1)} all-to-all(bf16[32,128,64]{1,2,0:T(8,128)(2,1)S(1)} %broadcast_in_dim.2), channel_id=1, replica_groups=mesh['band'=8,'ga'=32] {'ga'}, dimensions={0} | all-to-all | bytes 1048576 | tf_op jit(solution)/shard_map/all_to_all | solution.py:29
  206.4 0.0 copy-done.1
  206.4 0.0 copy-done.2
  206.4 7.3 %fusion = bf16[128,3072]{1,0:T(8,128)(2,1)} fusion(bf16[128,2048]{0,1:T(8,128)(2,1)S(1)} %bitcast.20, bf16[2048,3072]{1,0:T(8,128)(2,1)} %all-gather.2.cloned.1.call-done, bf16[128,3072]{1,0:T(8,128)(2,1)S(1)} %copy-done.1, f32[3072]{0:T(1024)S(1)} %copy-done.2), kind=kOutput, calls=%fused_computation.1 | convolution fusion | flops 1612185600 | bytes 14692352 | tf_op jit(solution)/shard_map/dot_general | solution.py:62
Async XLA Ops:
  6.5 160.3 %copy-start = (f32[4,8,8]{2,1,0:T(8,128)S(1)}, f32[4,8,8]{2,1,0:T(8,128)}, u32[]{:S(2)}) copy-start(f32[4,8,8]{2,1,0:T(8,128)} %param.9) | copy-start | bytes 3076
  6.5 199.9 %copy-start.1 = (bf16[128,3072]{1,0:T(8,128)(2,1)S(1)}, bf16[128,3072]{1,0:T(8,128)(2,1)}, u32[]{:S(2)}) copy-start(bf16[128,3072]{1,0:T(8,128)(2,1)} %param.5) | copy-start | bytes 2359300
  6.5 160.2 %copy-start.3 = (s32[256]{0:T(256)S(1)}, s32[256]{0:T(256)}, u32[]{:S(2)}) copy-start(s32[256]{0:T(256)} %param.8) | copy-start | bytes 3076
  6.5 199.9 %copy-start.2 = (f32[3072]{0:T(1024)S(1)}, f32[3072]{0:T(1024)}, u32[]{:S(2)}) copy-start(f32[3072]{0:T(1024)} %param.7) | copy-start | bytes 36868
  6.5 139.9 %all-gather.2.cloned.1.call-start = ((), (), s32[]{:S(2)}) async-start(), calls=%async_computation.2 | async-start | bytes 14155776 | tf_op jit(solution)/shard_map/all_gather | solution.py:57
  156.6 27.0 %all-to-all-start = ((bf16[32,128,64]{1,2,0:T(8,128)(2,1)}), bf16[32,128,64]{1,2,0:T(8,128)(2,1)S(1)}, u32[]{:S(2)}, u32[]{:S(2)}) async-start(bf16[32,128,64]{1,2,0:T(8,128)(2,1)} %bitcast.2), calls=%async_computation | async-start | bytes 1048576 | tf_op jit(solution)/shard_map/all_to_all | solution.py:17
Sparse Core Ops, SparseCore 0:
  9.1 137.3 all-gather.1
where the time goes:
time: 221 us
  waiting for transfers between devices  156 us (71%)
  blocking collectives  22.5 us (10%)
  matrix products  16.7 us (8%)
  between operations  13.5 us (6%)
  starting transfers between devices  10.2 us (5%)
    all_gather x1, waiting for transfers between devices, local(): all_proj = lax.all_gather(projectors, 'band', axis=0, tiled=True)  139 us
    all_to_all x1, blocking collectives, sent_to_all(): return lax.all_to_all(copies, axis, split_axis=0, concat_axis=0, tiled=True)  22.5 us
    all_to_all x1, waiting for transfers between devices, summed_on_arrival(): lax.all_to_all(in_blocks(array, dim, length), axis, 0, 0, tiled=True)  16.6 us
    all_to_all x1, starting transfers between devices, summed_on_arrival(): lax.all_to_all(in_blocks(array, dim, length), axis, 0, 0, tiled=True)  10.2 us
    dot_general x1, matrix products, local(): jnp.einsum('bg,pg->bp', wavefunctions, all_proj, preferred_element_type=j...  9.1 us
    dot_general x1, matrix products, local(): nonlocal_term = jnp.dot(mixed, all_proj, preferred_element_type=jnp.float32)  7.32 us
  transfers between devices with their start and end apart: 2, of which 2 were waited for; matrix products, arithmetic and copies ran while one was open for 0% of the time, Pallas kernels for 0%

commit v1 on v0

v1 whole, which is shorter than its diff:
```python
import functools

import jax
import jax.numpy as jnp
from jax import lax
from jax.experimental import pallas as pl
from jax.experimental.pallas import tpu as pltpu
from jax.sharding import PartitionSpec as P

NPA = 8
NX = 4
NZ = 8
MESH = pl.DeviceIdType.MESH
CUTS = ((0, 384), (384, 128))
W0R, W1R, W1L, W0L, FR, FL, P0, P1 = range(8)
RSY, AGY, RSZ, AGZ = 8, 10, 12, 14
T2A, T2B, RB, LA, ACA, ACB = range(16, 22)
COPIES = 22


def kernel(
    w_hbm,
    p_hbm,
    kin_ref,
    mt_ref,
    out_ref,
    wbuf,
    pbuf,
    c0,
    c1,
    r0,
    r1,
    sums,
    ysend,
    yrecv,
    dpair,
    dall,
    part_send,
    part_recv,
    own,
    block_diag,
    send_sem,
    recv_sem,
    load_sem,
):
    band = lax.axis_index("band")
    ga = lax.axis_index("ga")
    rows, cols = w_hbm.shape
    prows = p_hbm.shape[0]
    half_rows = rows // 2
    half = cols // 2
    x = lax.rem(band, NX)
    y_lo = band // NX
    core = lax.rem(ga, 2)
    y_hi = lax.rem(ga // 2, 2)
    z = ga // 4
    peer = z * 2 + core
    right = (y_lo * NX + lax.rem(x + 1, NX), ga)
    left = (y_lo * NX + lax.rem(x + NX - 1, NX), ga)
    across = ((1 - y_lo) * NX + x, ga)
    far = (band, (z * 2 + 1 - y_hi) * 2 + core)
    npeers = NZ * 2

    def peer_device(k):
        q = lax.rem(peer + k, npeers)
        return q, (band, ((q // 2) * 2 + y_hi) * 2 + lax.rem(q, 2))

    def copy(index, src, dst, device):
        return pltpu.make_async_remote_copy(
            src_ref=src,
            dst_ref=dst,
            send_sem=send_sem.at[index],
            recv_sem=recv_sem.at[index],
            device_id=device,
            device_id_type=MESH,
        )

    load_w = pltpu.make_async_copy(w_hbm, wbuf.at[pl.ds(0, rows)], load_sem.at[0])
    load_p = pltpu.make_async_copy(p_hbm, pbuf.at[pl.ds(0, prows)], load_sem.at[1])
    load_w.start()
    load_p.start()

    barrier = pltpu.get_barrier_semaphore()
    for device in (right, left, across, far):
        pl.semaphore_signal(barrier, inc=1, device_id=device, device_id_type=MESH)

    @pl.loop(1, npeers)
    def _(k):
        _, device = peer_device(k)
        pl.semaphore_signal(barrier, inc=1, device_id=device, device_id_type=MESH)

    pl.semaphore_wait(barrier, 4 + npeers - 1)

    low, high = pl.ds(0, half_rows), pl.ds(half_rows, half_rows)
    wrow = lambda block, part: pl.ds(block * rows + part * half_rows, half_rows)
    p0 = copy(P0, p_hbm.at[pl.ds(0, prows // 2)], pbuf.at[pl.ds(prows, prows // 2)], across)
    p1 = copy(
        P1,
        p_hbm.at[pl.ds(prows // 2, prows // 2)],
        pbuf.at[pl.ds(prows + prows // 2, prows // 2)],
        across,
    )
    w0r = copy(W0R, w_hbm.at[low], wbuf.at[wrow(1, 0)], right)
    w1r = copy(W1R, w_hbm.at[high], wbuf.at[wrow(1, 1)], right)
    w1l = copy(W1L, w_hbm.at[high], wbuf.at[wrow(2, 1)], left)
    w0l = copy(W0L, w_hbm.at[low], wbuf.at[wrow(2, 0)], left)
    fr = copy(FR, wbuf.at[wrow(1, 0)], wbuf.at[wrow(3, 0)], right)
    fl = copy(FL, wbuf.at[wrow(2, 1)], wbuf.at[wrow(3, 1)], left)
    for c in (w0r, w1l, p0, w1r, w0l, p1):
        c.start()

    starts = (
        band * prows,
        band * prows + 128,
        across[0] * prows,
        across[0] * prows + 128,
    )
    q_at = lax.broadcasted_iota(jnp.int32, (128, 128), 0) // NPA
    p_at = lax.broadcasted_iota(jnp.int32, (128, 128), 1) // NPA
    for b, start in enumerate(starts):
        strip = mt_ref[:, pl.ds(pl.multiple_of(start, 128), 128)]
        tiled = jnp.concatenate([strip] * (128 // NPA), axis=0)
        block_diag[pl.ds(b * 128, 128), :] = jnp.where(q_at == p_at, tiled, 0.0)

    cbuf, rbuf = (c0, c1), (r0, r1)

    def correlate(row, count, pstart, pcount, target, tcol):
        c = lax.dot_general(
            wbuf[pl.ds(row, count), :],
            pbuf[pl.ds(pstart, pcount), :],
            (((1,), (1,)), ((), ())),
            preferred_element_type=jnp.float32,
        )
        target[pl.ds(row, count), pl.ds(tcol, pcount)] = c.astype(jnp.bfloat16)

    load_w.wait()
    load_p.wait()
    correlate(0, rows, 0, prows, c0, 0)
    w0r.wait_recv()
    fr.start()
    w1l.wait_recv()
    fl.start()
    w1r.wait_recv()
    w0l.wait_recv()
    correlate(rows, 2 * rows, 0, prows, c0, 0)
    p0.wait_recv()
    correlate(0, 3 * rows, prows, prows // 2, c0, prows)
    fr.wait_recv()
    fl.wait_recv()
    correlate(3 * rows, rows, 0, prows + prows // 2, c0, 0)

    share = 4 * rows // npeers
    hshare = share // 2

    def scatter_start(i):
        @pl.loop(1, npeers)
        def _(k):
            q, device = peer_device(k)
            copy(
                RSZ + i,
                cbuf[i].at[pl.ds(pl.multiple_of(q * share, share), share)],
                rbuf[i].at[pl.ds(pl.multiple_of(peer * share, share), share)],
                device,
            ).start()

        here = pl.ds(pl.multiple_of(peer * share, share), share)
        rbuf[i][here, :] = cbuf[i][here, :]

    def many(index, ref):
        return copy(index, ref, ref, right)

    keep = pl.ds(pl.multiple_of(y_hi * hshare, hshare), hshare)
    give = pl.ds(pl.multiple_of((1 - y_hi) * hshare, hshare), hshare)
    rest = pl.ds(0, (npeers - 1) * share)

    def y_sum(i):
        start, width = CUTS[i]
        at = pl.ds(start, width)
        return copy(RSY + i, ysend.at[:, at], yrecv.at[:, at], far)

    def y_share(i):
        start, width = CUTS[i]
        at = pl.ds(start, width)
        return copy(AGY + i, dpair.at[keep, at], dpair.at[keep, at], far)

    def scatter_sum(i):
        start, width = CUTS[i]
        at = pl.ds(start, width)
        many(RSZ + i, rbuf[i].at[rest]).wait_recv()
        total = rbuf[i][pl.ds(0, share), :].astype(jnp.float32)
        for q in range(1, npeers):
            total += rbuf[i][pl.ds(q * share, share), :].astype(jnp.float32)
        sums[:, at] = total
        ysend[:, at] = sums[give, at].astype(jnp.bfloat16)
        y_sum(i).start()

    def couple(i):
        start, width = CUTS[i]
        y_sum(i).wait_recv()
        for b in range(start // 128, (start + width) // 128):
            at = pl.ds(b * 128, 128)
            total = sums[keep, at] + yrecv[:, at].astype(jnp.float32)
            mixed = jnp.dot(
                total,
                block_diag[at, :],
                precision=lax.Precision.HIGHEST,
                preferred_element_type=jnp.float32,
            )
            dpair[keep, at] = mixed.astype(jnp.bfloat16)
        y_share(i).start()

    def gather_start(i):
        start, width = CUTS[i]
        at = pl.ds(start, width)
        y_share(i).wait_recv()
        here = pl.ds(pl.multiple_of(peer * share, share), share)

        @pl.loop(1, npeers)
        def _(k):
            _, device = peer_device(k)
            copy(AGZ + i, dpair.at[:, at], dall.at[here, at], device).start()

        dall[here, at] = dpair[:, at]

    scatter_start(0)
    p1.wait_recv()
    correlate(0, 4 * rows, prows + prows // 2, prows // 2, c1, 0)
    scatter_start(1)
    scatter_sum(0)
    couple(0)
    gather_start(0)
    scatter_sum(1)
    couple(1)
    gather_start(1)
    for i in range(2):
        start, width = CUTS[i]
        many(AGZ + i, dall.at[rest, pl.ds(start, width)]).wait_recv()

    def partial(block, side):
        return jnp.dot(
            dall[pl.ds(block * rows, rows), :],
            pbuf[:, pl.ds(side * half, half)],
            preferred_element_type=jnp.float32,
        )

    def send_part(index, device):
        slot = index - T2A
        return copy(index, part_send.at[slot], part_recv.at[slot], device)

    t2a, t2b = send_part(T2A, right), send_part(T2B, left)
    rb, la = send_part(RB, right), send_part(LA, left)
    aca, acb = send_part(ACA, right), send_part(ACB, left)

    def put(index, value):
        part_send[index - T2A] = value.astype(jnp.bfloat16)

    def got(index):
        return part_recv[index - T2A].astype(jnp.float32)

    put(T2A, partial(3, 0))
    t2a.start()
    put(T2B, partial(3, 1))
    t2b.start()
    put(RB, partial(2, 1))
    rb.start()
    put(LA, partial(1, 0))
    la.start()
    own[:, pl.ds(0, half)] = partial(2, 0)
    own[:, pl.ds(half, half)] = partial(1, 1)
    t2a.wait_recv()
    put(ACA, own[:, pl.ds(0, half)] + got(T2A))
    aca.start()
    t2b.wait_recv()
    put(ACB, own[:, pl.ds(half, half)] + got(T2B))
    acb.start()
    for side in range(2):
        at = pl.ds(side * half, half)
        own[:, at] = partial(0, side) + kin_ref[:, at] * wbuf[pl.ds(0, rows), at].astype(
            jnp.float32
        )
    la.wait_recv()
    own[:, pl.ds(0, half)] += got(LA)
    rb.wait_recv()
    own[:, pl.ds(half, half)] += got(RB)
    aca.wait_recv()
    out_ref[:, pl.ds(0, half)] = (own[:, pl.ds(0, half)] + got(ACA)).astype(jnp.bfloat16)
    acb.wait_recv()
    out_ref[:, pl.ds(half, half)] = (own[:, pl.ds(half, half)] + got(ACB)).astype(jnp.bfloat16)

    for c in (w0r, w1r, w1l, w0l, fr, fl, p0, p1, t2a, t2b, rb, la, aca, acb):
        c.wait_send()
    for i in range(2):
        start, width = CUTS[i]
        y_sum(i).wait_send()
        y_share(i).wait_send()
        many(RSZ + i, rbuf[i].at[rest]).wait_send()
        many(AGZ + i, dall.at[rest, pl.ds(start, width)]).wait_send()


def local(wavefunctions, projectors, kinetic_diag, species_index, coupling):
    rows, cols = wavefunctions.shape
    prows = projectors.shape[0]
    width = 2 * prows
    bf16, f32 = jnp.bfloat16, jnp.float32
    turned = coupling.transpose(0, 2, 1)
    picked = jnp.zeros((NPA, species_index.shape[0], NPA), f32)
    for k in range(coupling.shape[0]):
        picked = jnp.where(
            (species_index == k)[None, :, None], turned[k][:, None, :], picked
        )
    mt = picked.reshape(NPA, species_index.shape[0] * NPA)
    share = 4 * rows // (2 * NZ)
    vmem = pl.BlockSpec(memory_space=pltpu.VMEM)
    anywhere = pl.BlockSpec(memory_space=pl.ANY)
    return pl.pallas_call(
        kernel,
        out_shape=jax.ShapeDtypeStruct((rows, cols), bf16),
        in_specs=[anywhere, anywhere, vmem, vmem],
        out_specs=vmem,
        scratch_shapes=[
            pltpu.VMEM((4 * rows, cols), bf16),
            pltpu.VMEM((width, cols), bf16),
            pltpu.VMEM((4 * rows, CUTS[0][1]), bf16),
            pltpu.VMEM((4 * rows, CUTS[1][1]), bf16),
            pltpu.VMEM((4 * rows, CUTS[0][1]), bf16),
            pltpu.VMEM((4 * rows, CUTS[1][1]), bf16),
            pltpu.VMEM((share, width), f32),
            pltpu.VMEM((share // 2, width), bf16),
            pltpu.VMEM((share // 2, width), bf16),
            pltpu.VMEM((share, width), bf16),
            pltpu.VMEM((4 * rows, width), bf16),
            pltpu.VMEM((6, rows, cols // 2), bf16),
            pltpu.VMEM((6, rows, cols // 2), bf16),
            pltpu.VMEM((rows, cols), f32),
            pltpu.VMEM((width, 128), f32),
            pltpu.SemaphoreType.DMA((COPIES,)),
            pltpu.SemaphoreType.DMA((COPIES,)),
            pltpu.SemaphoreType.DMA((2,)),
        ],
        compiler_params=pltpu.CompilerParams(
            collective_id=0, has_side_effects=True, vmem_limit_bytes=48 * 1024 * 1024
        ),
    )(wavefunctions, projectors, kinetic_diag.reshape(1, cols), mt)


def solution(mesh):
    in_specs = (P("band", "ga"), P("band", "ga"), P("ga"), P(), P())
    out_specs = P("band", "ga")
    return jax.shard_map(local, mesh=mesh, in_specs=in_specs, out_specs=out_specs, check_vma=False)
```

time: 221 us -> 110 us (0.50)
  the two profiles are of different devices: /device:TPU:1 before, /device:TPU:14 now
where the time goes in v1:
time: 110 us
  Pallas kernels  99.8 us (91%)
  local copies, waits for them, and re-layouts  8.47 us (8%)
  other arithmetic  1.6 us (1%)
    pallas_call x1, Pallas kernels, local(): pl.pallas_call(kernel, out_shape=jax.ShapeDtypeStruct((rows, cols), bf16)...  99.8 us
    broadcast_in_dim x17, local copies, waits for them, and re-layouts, local(): jnp.where((species_index == k)[None, :, None], turned[k][:, None, :], pic...  6.78 us

profile of v1, /device:TPU:14, one launch (start us, length us, event | category | flops | bytes accessed | tf_op | source)
XLA Modules:
  0.0 110.0 jit_solution(15376881710217287512)
XLA Ops:
  0.0 0.7 broadcast_compare_fusion.3
  0.7 0.8 copy.7
  1.5 0.1 broadcast_in_dim.85
  1.6 0.7 broadcast_in_dim.86
  2.3 0.1 broadcast_in_dim.91
  2.4 0.7 broadcast_in_dim.92
  3.1 0.1 broadcast_in_dim.103
  3.2 0.7 broadcast_in_dim.104
  3.9 0.1 broadcast_in_dim.97
  4.0 0.7 broadcast_in_dim.98
  4.7 0.1 broadcast_in_dim.107
  4.8 0.5 broadcast_in_dim.108
  5.3 0.1 broadcast_in_dim.101
  5.4 0.5 broadcast_in_dim.102
  5.9 0.1 broadcast_in_dim.95
  5.9 0.0 copy-start
  6.0 0.0 copy-start.1
  6.0 0.0 copy-start.2
  6.0 1.1 %broadcast_in_dim.96 = f32[8,2048]{1,0:T(8,128)} reshape(f32[8,256,8]{2,1,0:T(8,128)S(1)} %broadcast_in_dim.95) | data formatting | bytes 131072 | tf_op jit(solution)/shard_map/jit(_where)/broadcast_in_dim | solution.py:308
  7.1 0.1 broadcast_in_dim.89
  7.2 1.1 %broadcast_in_dim.90 = f32[8,2048]{1,0:T(8,128)} reshape(f32[8,256,8]{2,1,0:T(8,128)S(1)} %broadcast_in_dim.89) | data formatting | bytes 131072 | tf_op jit(solution)/shard_map/jit(_where)/broadcast_in_dim | solution.py:308
  8.3 0.9 select_select_fusion.mt_ref
  9.3 99.8 %shard_map.55 = bf16[128,3072]{1,0:T(8,128)(2,1)S(1)} custom-call(bf16[128,3072]{1,0:T(8,128)(2,1)S(1)} %copy-done.1, bf16[256,3072]{1,0:T(8,128)(2,1)S(1)} %copy-done, f32[1,3072]{1,0:T(1,128)S(1)} %bitcast.10, f32[8,2048]{1,0:T(8,128)S(1)} %select_select_fusion.mt_ref), custom_call_target="tpu_custom_call" | custom-call | tf_op jit(solution)/shard_map/pallas_call | solution.py:315
  109.1 0.9 copy.9
  (4 shorter events, 0.0 us)
Async XLA Ops:
  5.9 3.3 %copy-start = (bf16[256,3072]{1,0:T(8,128)(2,1)S(1)}, bf16[256,3072]{1,0:T(8,128)(2,1)}, u32[]{:S(2)}) copy-start(bf16[256,3072]{1,0:T(8,128)(2,1)} %p_hbm.1) | copy-start | bytes 4718596
  6.0 3.3 %copy-start.1 = (bf16[128,3072]{1,0:T(8,128)(2,1)S(1)}, bf16[128,3072]{1,0:T(8,128)(2,1)}, u32[]{:S(2)}) copy-start(bf16[128,3072]{1,0:T(8,128)(2,1)} %w_hbm.1) | copy-start | bytes 2359300
  6.0 3.3 %copy-start.2 = (f32[3072]{0:T(1024)S(1)}, f32[3072]{0:T(1024)}, u32[]{:S(2)}) copy-start(f32[3072]{0:T(1024)} %param.7) | copy-start | bytes 36868

commit v2 on v1

v2 whole, which is shorter than its diff:
```python
import jax
import jax.numpy as jnp
from jax import lax
from jax.experimental import pallas as pl
from jax.experimental.pallas import tpu as pltpu
from jax.sharding import PartitionSpec as P

NPA = 8
NX = 4
NZ = 8
MESH = pl.DeviceIdType.MESH
CUTS = ((0, 384), (384, 128))
W0R, W1R, W1L, W0L, FR, FL, P0, P1, RS0, RSY, RS1, AG0, AGC, AG1 = range(14)
T2A, T2B, RB, LA, ACA, ACB = range(14, 20)
COPIES = 20
ROUNDS = 4


def kernel(
    w_hbm,
    p_hbm,
    kin_hbm,
    species_hbm,
    coupling_ref,
    out_ref,
    wbuf,
    pbuf,
    c0,
    c1,
    r0,
    r1,
    sums,
    ysend,
    yrecv,
    dall,
    part_send,
    part_recv,
    own,
    block_diag,
    kin_ref,
    species,
    send_sem,
    recv_sem,
    load_sem,
    meet_sem,
):
    band = lax.axis_index("band")
    ga = lax.axis_index("ga")
    rows, cols = w_hbm.shape
    prows = p_hbm.shape[0]
    half_rows = rows // 2
    half = cols // 2
    x = lax.rem(band, NX)
    y_lo = band // NX
    core = lax.rem(ga, 2)
    y_hi = lax.rem(ga // 2, 2)
    z = ga // 4
    right = (y_lo * NX + lax.rem(x + 1, NX), ga)
    left = (y_lo * NX + lax.rem(x + NX - 1, NX), ga)
    across = ((1 - y_lo) * NX + x, ga)

    def at_place(z, y_hi, core):
        return (band, (z * 2 + y_hi) * 2 + core)

    far = at_place(z, 1 - y_hi, core)
    twin = at_place(z, y_hi, 1 - core)
    above = at_place(lax.rem(z + 1, NZ), y_hi, core)
    below = at_place(lax.rem(z + NZ - 1, NZ), y_hi, core)
    nga = 4 * NZ
    npeers = 2 * NZ
    peer = core * NZ + z

    def copy(index, src, dst, device):
        return pltpu.make_async_remote_copy(
            src_ref=src,
            dst_ref=dst,
            send_sem=send_sem.at[index],
            recv_sem=recv_sem.at[index],
            device_id=device,
            device_id_type=MESH,
        )

    load_w = pltpu.make_async_copy(w_hbm, wbuf.at[pl.ds(0, rows)], load_sem.at[0])
    load_p = pltpu.make_async_copy(p_hbm, pbuf.at[pl.ds(0, prows)], load_sem.at[1])
    load_kin = pltpu.make_async_copy(kin_hbm, kin_ref, load_sem.at[2])
    load_species = pltpu.make_async_copy(species_hbm, species, load_sem.at[3])
    for c in (load_species, load_w, load_p, load_kin):
        c.start()

    barrier = pltpu.get_barrier_semaphore()
    near = (right, left, across, far, twin, above, below)
    for device in near:
        pl.semaphore_signal(barrier, inc=1, device_id=device, device_id_type=MESH)
    pl.semaphore_wait(barrier, len(near))

    low, high = pl.ds(0, half_rows), pl.ds(half_rows, half_rows)
    wrow = lambda block, part: pl.ds(block * rows + part * half_rows, half_rows)
    p0 = copy(P0, p_hbm.at[pl.ds(0, prows // 2)], pbuf.at[pl.ds(prows, prows // 2)], across)
    p1 = copy(
        P1,
        p_hbm.at[pl.ds(prows // 2, prows // 2)],
        pbuf.at[pl.ds(prows + prows // 2, prows // 2)],
        across,
    )
    w0r = copy(W0R, w_hbm.at[low], wbuf.at[wrow(1, 0)], right)
    w1r = copy(W1R, w_hbm.at[high], wbuf.at[wrow(1, 1)], right)
    w1l = copy(W1L, w_hbm.at[high], wbuf.at[wrow(2, 1)], left)
    w0l = copy(W0L, w_hbm.at[low], wbuf.at[wrow(2, 0)], left)
    fr = copy(FR, wbuf.at[wrow(1, 0)], wbuf.at[wrow(3, 0)], right)
    fl = copy(FL, wbuf.at[wrow(2, 1)], wbuf.at[wrow(3, 1)], left)
    for c in (w0r, w1l, p0, w1r, w0l, p1):
        c.start()

    load_species.wait()
    lane = lax.broadcasted_iota(jnp.int32, (NPA, 128), 1)
    index_at = lax.broadcasted_iota(jnp.int32, (NPA, 128), 0)
    spread = jnp.where(lax.rem(lane, NPA) == index_at, 1.0, 0.0).astype(jnp.float32)
    turned = [
        lax.dot_general(
            coupling_ref[k],
            spread,
            (((0,), (0,)), ((), ())),
            precision=lax.Precision.HIGHEST,
            preferred_element_type=jnp.float32,
        )
        for k in range(coupling_ref.shape[0])
    ]
    q_at = lax.broadcasted_iota(jnp.int32, (128, 128), 0) // NPA
    p_at = lax.broadcasted_iota(jnp.int32, (128, 128), 1) // NPA
    per_block = 128 // NPA
    atoms = prows // NPA
    for b in range(4):
        first = (band if b < 2 else across[0]) * atoms + (b % 2) * per_block
        kinds = jnp.zeros((NPA, 128), jnp.int32)
        for a in range(per_block):
            kinds = jnp.where(lane // NPA == a, species[first + a], kinds)
        strip = jnp.zeros((NPA, 128), jnp.float32)
        for k, matrix in enumerate(turned):
            strip = jnp.where(kinds == k, matrix, strip)
        tiled = jnp.concatenate([strip] * per_block, axis=0)
        block_diag[pl.ds(b * 128, 128), :] = jnp.where(q_at == p_at, tiled, 0.0)

    for i in range(ROUNDS):
        for device in (above, below):
            pl.semaphore_signal(
                meet_sem.at[i], inc=1, device_id=device, device_id_type=MESH
            )
        pl.semaphore_wait(meet_sem.at[i], 2)
    pl.semaphore_signal(
        meet_sem.at[ROUNDS], inc=1, device_id=twin, device_id_type=MESH
    )
    pl.semaphore_wait(meet_sem.at[ROUNDS], 1)

    def correlate(row, count, pstart, pcount, target, tcol):
        c = lax.dot_general(
            wbuf[pl.ds(row, count), :],
            pbuf[pl.ds(pstart, pcount), :],
            (((1,), (1,)), ((), ())),
            preferred_element_type=jnp.float32,
        )
        target[pl.ds(row, count), pl.ds(tcol, pcount)] = c.astype(jnp.bfloat16)

    share = 4 * rows // npeers
    piece = share // 2
    mine = pl.ds(pl.multiple_of((peer * 2 + y_hi) * piece, piece), piece)
    keep = pl.ds(pl.multiple_of(y_hi * piece, piece), piece)
    give = pl.ds(pl.multiple_of((1 - y_hi) * piece, piece), piece)
    first, last = (pl.ds(*cut) for cut in CUTS)

    def many(index, ref):
        return copy(index, ref, ref, right)

    all_rs0 = many(RS0, r0.at[pl.ds(0, (npeers - 1) * share)])
    all_rs1 = many(RS1, r1.at[pl.ds(0, (nga - 1) * piece)])
    all_ag0 = many(AG0, dall.at[pl.ds(0, (npeers - 1) * piece), first])
    all_ag1 = many(AG1, dall.at[pl.ds(0, (nga - 1) * piece), last])

    def scatter_first(low, count):
        @pl.loop(0, count)
        def _(k):
            q = low + lax.rem(peer + k, count)

            @pl.when(q != peer)
            def _():
                copy(
                    RS0,
                    c0.at[pl.ds(pl.multiple_of(q * share, share), share)],
                    r0.at[pl.ds(pl.multiple_of(peer * share, share), share)],
                    at_place(lax.rem(q, NZ), y_hi, q // NZ),
                ).start()

    def other(k):
        g = lax.rem(ga + k, nga)
        place = (g // 4, lax.rem(g // 2, 2), lax.rem(g, 2))
        row = ((place[2] * NZ + place[0]) * 2 + place[1]) * piece
        return pl.ds(pl.multiple_of(row, piece), piece), at_place(*place)

    def couple(total, b):
        return jnp.dot(
            total,
            block_diag[pl.ds(b * 128, 128), :],
            precision=lax.Precision.HIGHEST,
            preferred_element_type=jnp.float32,
        ).astype(jnp.bfloat16)

    load_w.wait()
    load_p.wait()
    correlate(0, rows, 0, prows, c0, 0)
    w0r.wait_recv()
    fr.start()
    w1l.wait_recv()
    fl.start()
    w1r.wait_recv()
    w0l.wait_recv()
    correlate(rows, 2 * rows, 0, prows, c0, 0)
    p0.wait_recv()
    correlate(0, 3 * rows, prows, prows // 2, c0, prows)
    early = 3 * npeers // 4
    scatter_first(0, early)
    fr.wait_recv()
    fl.wait_recv()
    correlate(3 * rows, rows, 0, prows + prows // 2, c0, 0)
    scatter_first(early, npeers - early)
    here = pl.ds(pl.multiple_of(peer * share, share), share)
    r0[here, :] = c0[here, :]

    p1.wait_recv()
    correlate(0, 4 * rows, prows + prows // 2, prows // 2, c1, 0)

    @pl.loop(1, nga)
    def _(k):
        at, device = other(k)
        copy(RS1, c1.at[at], r1.at[mine], device).start()

    r1[mine, :] = c1[mine, :]

    all_rs0.wait_recv()
    total = r0[pl.ds(0, share), :].astype(jnp.float32)
    for q in range(1, npeers):
        total += r0[pl.ds(q * share, share), :].astype(jnp.float32)
    sums[...] = total
    ysend[...] = sums[give, :].astype(jnp.bfloat16)
    y_sum = copy(RSY, ysend, yrecv, far)
    y_sum.start()
    y_sum.wait_recv()
    for b in range(CUTS[0][1] // 128):
        at = pl.ds(b * 128, 128)
        dall[mine, at] = couple(sums[keep, at] + yrecv[:, at].astype(jnp.float32), b)

    @pl.loop(1, npeers)
    def _(k):
        j = lax.rem(z * 2 + y_hi + k, npeers)
        device = at_place(j // 2, lax.rem(j, 2), core)
        copy(AG0, dall.at[mine, first], dall.at[mine, first], device).start()

    all_rs1.wait_recv()
    total = r1[pl.ds(0, piece), :].astype(jnp.float32)
    for q in range(1, nga):
        total += r1[pl.ds(q * piece, piece), :].astype(jnp.float32)
    dall[mine, last] = couple(total, 3)

    @pl.loop(1, nga)
    def _(k):
        _, device = other(k)
        copy(AG1, dall.at[mine, last], dall.at[mine, last], device).start()

    all_ag0.wait_recv()
    half_block = pl.ds(pl.multiple_of(core * 2 * rows, 2 * rows), 2 * rows)
    to_twin = copy(AGC, dall.at[half_block, first], dall.at[half_block, first], twin)
    to_twin.start()
    to_twin.wait_recv()
    all_ag1.wait_recv()

    def partial(block, side):
        return jnp.dot(
            dall[pl.ds(block * rows, rows), :],
            pbuf[:, pl.ds(side * half, half)],
            preferred_element_type=jnp.float32,
        )

    def send_part(index, device):
        slot = index - T2A
        return copy(index, part_send.at[slot], part_recv.at[slot], device)

    t2a, t2b = send_part(T2A, right), send_part(T2B, left)
    rb, la = send_part(RB, right), send_part(LA, left)
    aca, acb = send_part(ACA, right), send_part(ACB, left)

    def put(index, value):
        part_send[index - T2A] = value.astype(jnp.bfloat16)

    def got(index):
        return part_recv[index - T2A].astype(jnp.float32)

    put(T2A, partial(3, 0))
    t2a.start()
    put(T2B, partial(3, 1))
    t2b.start()
    put(RB, partial(2, 1))
    rb.start()
    put(LA, partial(1, 0))
    la.start()
    own[:, pl.ds(0, half)] = partial(2, 0)
    own[:, pl.ds(half, half)] = partial(1, 1)
    t2a.wait_recv()
    put(ACA, own[:, pl.ds(0, half)] + got(T2A))
    aca.start()
    t2b.wait_recv()
    put(ACB, own[:, pl.ds(half, half)] + got(T2B))
    acb.start()
    load_kin.wait()
    for side in range(2):
        at = pl.ds(side * half, half)
        own[:, at] = partial(0, side) + kin_ref[:, at] * wbuf[pl.ds(0, rows), at].astype(
            jnp.float32
        )
    la.wait_recv()
    own[:, pl.ds(0, half)] += got(LA)
    rb.wait_recv()
    own[:, pl.ds(half, half)] += got(RB)
    aca.wait_recv()
    out_ref[:, pl.ds(0, half)] = (own[:, pl.ds(0, half)] + got(ACA)).astype(jnp.bfloat16)
    acb.wait_recv()
    out_ref[:, pl.ds(half, half)] = (own[:, pl.ds(half, half)] + got(ACB)).astype(jnp.bfloat16)

    for c in (w0r, w1r, w1l, w0l, fr, fl, p0, p1, y_sum, to_twin, t2a, t2b, rb, la, aca, acb):
        c.wait_send()
    for c in (all_rs0, all_rs1, all_ag0, all_ag1):
        c.wait_send()


def local(wavefunctions, projectors, kinetic_diag, species_index, coupling):
    rows, cols = wavefunctions.shape
    prows = projectors.shape[0]
    width = 2 * prows
    bf16, f32 = jnp.bfloat16, jnp.float32
    share = 4 * rows // (2 * NZ)
    vmem = pl.BlockSpec(memory_space=pltpu.VMEM)
    anywhere = pl.BlockSpec(memory_space=pl.ANY)
    return pl.pallas_call(
        kernel,
        out_shape=jax.ShapeDtypeStruct((rows, cols), bf16),
        in_specs=[anywhere, anywhere, anywhere, anywhere, vmem],
        out_specs=vmem,
        scratch_shapes=[
            pltpu.VMEM((4 * rows, cols), bf16),
            pltpu.VMEM((width, cols), bf16),
            pltpu.VMEM((4 * rows, CUTS[0][1]), bf16),
            pltpu.VMEM((4 * rows, CUTS[1][1]), bf16),
            pltpu.VMEM((4 * rows, CUTS[0][1]), bf16),
            pltpu.VMEM((4 * rows, CUTS[1][1]), bf16),
            pltpu.VMEM((share, CUTS[0][1]), f32),
            pltpu.VMEM((share // 2, CUTS[0][1]), bf16),
            pltpu.VMEM((share // 2, CUTS[0][1]), bf16),
            pltpu.VMEM((4 * rows, width), bf16),
            pltpu.VMEM((6, rows, cols // 2), bf16),
            pltpu.VMEM((6, rows, cols // 2), bf16),
            pltpu.VMEM((rows, cols), f32),
            pltpu.VMEM((width, 128), f32),
            pltpu.VMEM((1, cols), f32),
            pltpu.SMEM(species_index.shape, jnp.int32),
            pltpu.SemaphoreType.DMA((COPIES,)),
            pltpu.SemaphoreType.DMA((COPIES,)),
            pltpu.SemaphoreType.DMA((4,)),
            pltpu.SemaphoreType.REGULAR((ROUNDS + 1,)),
        ],
        compiler_params=pltpu.CompilerParams(
            collective_id=0, has_side_effects=True, vmem_limit_bytes=67043328
        ),
    )(wavefunctions, projectors, kinetic_diag.reshape(1, cols), species_index, coupling)


def solution(mesh):
    in_specs = (P("band", "ga"), P("band", "ga"), P("ga"), P(), P())
    out_specs = P("band", "ga")
    return jax.shard_map(local, mesh=mesh, in_specs=in_specs, out_specs=out_specs, check_vma=False)
```

time: 110 us -> 93.4 us (0.85)
  the two profiles are of different devices: /device:TPU:14 before, /device:TPU:1 now
where the time goes in v2:
time: 93.4 us; the launch traced here: 93.2 us
  Pallas kernels  91.1 us (98%)
  local copies, waits for them, and re-layouts  2.06 us (2%)
    pallas_call x1, Pallas kernels, local(): pl.pallas_call(kernel, out_shape=jax.ShapeDtypeStruct((rows, cols), bf16)...  91.1 us
    unnamed x1, local copies, waits for them, and re-layouts  2.06 us

profile of v2, /device:TPU:1, one launch (start us, length us, event | category | flops | bytes accessed | tf_op | source)
XLA Modules:
  0.0 93.2 jit_solution(13294400835000388679)
XLA Ops:
  0.0 91.1 %shard_map.55 = bf16[128,3072]{1,0:T(8,128)(2,1)} custom-call(bf16[128,3072]{1,0:T(8,128)(2,1)} %w_hbm.1, bf16[256,3072]{1,0:T(8,128)(2,1)} %p_hbm.1, f32[1,3072]{1,0:T(1,128)} %bitcast.1, s32[256]{0:T(256)} %species_hbm.1, f32[4,8,8]{2,1,0:T(8,128)} %coupling_ref.1), custom_call_target="tpu_custom_call" | custom-call | tf_op jit(solution)/shard_map/pallas_call | solution.py:340
  91.1 2.1 %copy.7 = bf16[128,3072]{1,0:T(8,128)(2,1)} copy(bf16[128,3072]{1,0:T(8,128)(2,1)} %shard_map.55) | data formatting | bytes 1572864

commit v3 on v2

--- a/solution.py
+++ b/solution.py
@@ -11,8 +11,8 @@
 MESH = pl.DeviceIdType.MESH
 CUTS = ((0, 384), (384, 128))
 W0R, W1R, W1L, W0L, FR, FL, P0, P1, RS0, RSY, RS1, AG0, AGC, AG1 = range(14)
-T2A, T2B, RB, LA, ACA, ACB = range(14, 20)
-COPIES = 20
+T2A, T2B, RB, LA, ACA, ACB = range(14, 26, 2)
+COPIES = 26
 ROUNDS = 4
 
 
@@ -190,8 +190,13 @@
                 ).start()
 
     def other(k):
-        g = lax.rem(ga + k, nga)
-        place = (g // 4, lax.rem(g // 2, 2), lax.rem(g, 2))
+        i = k // 4
+        d = NZ // 2 + jnp.where(lax.rem(i, 2) == 0, i // 2, -((i + 1) // 2))
+        place = (
+            lax.rem(z + d, NZ),
+            lax.rem(y_hi + 1 - lax.rem(k, 4) // 2, 2),
+            lax.rem(core + 1 - lax.rem(k, 2), 2),
+        )
         row = ((place[2] * NZ + place[0]) * 2 + place[1]) * piece
         return pl.ds(pl.multiple_of(row, piece), piece), at_place(*place)
 
@@ -224,16 +229,6 @@
     here = pl.ds(pl.multiple_of(peer * share, share), share)
     r0[here, :] = c0[here, :]
 
-    p1.wait_recv()
-    correlate(0, 4 * rows, prows + prows // 2, prows // 2, c1, 0)
-
-    @pl.loop(1, nga)
-    def _(k):
-        at, device = other(k)
-        copy(RS1, c1.at[at], r1.at[mine], device).start()
-
-    r1[mine, :] = c1[mine, :]
-
     all_rs0.wait_recv()
     total = r0[pl.ds(0, share), :].astype(jnp.float32)
     for q in range(1, npeers):
@@ -242,15 +237,24 @@
     ysend[...] = sums[give, :].astype(jnp.bfloat16)
     y_sum = copy(RSY, ysend, yrecv, far)
     y_sum.start()
+    p1.wait_recv()
+    correlate(0, 4 * rows, prows + prows // 2, prows // 2, c1, 0)
+
+    @pl.loop(0, nga - 1)
+    def _(k):
+        at, device = other(k)
+        copy(RS1, c1.at[at], r1.at[mine], device).start()
+
+    r1[mine, :] = c1[mine, :]
+
     y_sum.wait_recv()
     for b in range(CUTS[0][1] // 128):
         at = pl.ds(b * 128, 128)
         dall[mine, at] = couple(sums[keep, at] + yrecv[:, at].astype(jnp.float32), b)
 
-    @pl.loop(1, npeers)
+    @pl.loop(0, npeers - 1)
     def _(k):
-        j = lax.rem(z * 2 + y_hi + k, npeers)
-        device = at_place(j // 2, lax.rem(j, 2), core)
+        _, device = other(2 * k + 1)
         copy(AG0, dall.at[mine, first], dall.at[mine, first], device).start()
 
     all_rs1.wait_recv()
@@ -259,7 +263,7 @@
         total += r1[pl.ds(q * piece, piece), :].astype(jnp.float32)
     dall[mine, last] = couple(total, 3)
 
-    @pl.loop(1, nga)
+    @pl.loop(0, nga - 1)
     def _(k):
         _, device = other(k)
         copy(AG1, dall.at[mine, last], dall.at[mine, last], device).start()
@@ -271,59 +275,70 @@
     to_twin.wait_recv()
     all_ag1.wait_recv()
 
-    def partial(block, side):
+    quarter = half // 2
+
+    def send_part(index, sub, device):
+        slot = (index - T2A) // 2
+        at = pl.ds(sub * quarter, quarter)
+        return copy(
+            index + sub, part_send.at[slot, :, at], part_recv.at[slot, :, at], device
+        )
+
+    def partial(block, side, sub):
         return jnp.dot(
             dall[pl.ds(block * rows, rows), :],
-            pbuf[:, pl.ds(side * half, half)],
+            pbuf[:, pl.ds(side * half + sub * quarter, quarter)],
             preferred_element_type=jnp.float32,
         )
 
-    def send_part(index, device):
-        slot = index - T2A
-        return copy(index, part_send.at[slot], part_recv.at[slot], device)
-
-    t2a, t2b = send_part(T2A, right), send_part(T2B, left)
-    rb, la = send_part(RB, right), send_part(LA, left)
-    aca, acb = send_part(ACA, right), send_part(ACB, left)
-
-    def put(index, value):
-        part_send[index - T2A] = value.astype(jnp.bfloat16)
-
-    def got(index):
-        return part_recv[index - T2A].astype(jnp.float32)
-
-    put(T2A, partial(3, 0))
-    t2a.start()
-    put(T2B, partial(3, 1))
-    t2b.start()
-    put(RB, partial(2, 1))
-    rb.start()
-    put(LA, partial(1, 0))
-    la.start()
-    own[:, pl.ds(0, half)] = partial(2, 0)
-    own[:, pl.ds(half, half)] = partial(1, 1)
-    t2a.wait_recv()
-    put(ACA, own[:, pl.ds(0, half)] + got(T2A))
-    aca.start()
-    t2b.wait_recv()
-    put(ACB, own[:, pl.ds(half, half)] + got(T2B))
-    acb.start()
+    def put(index, sub, value):
+        part_send[(index - T2A) // 2, :, pl.ds(sub * quarter, quarter)] = value.astype(
+            jnp.bfloat16
+        )
+
+    def got(index, sub):
+        return part_recv[(index - T2A) // 2, :, pl.ds(sub * quarter, quarter)].astype(
+            jnp.float32
+        )
+
+    targets = {T2A: right, RB: right, ACA: right, T2B: left, LA: left, ACB: left}
+    parts = {(i, sub): send_part(i, sub, targets[i]) for i in targets for sub in range(2)}
+    for index, index2, block, block2 in ((T2A, T2B, 3, 3), (RB, LA, 2, 1)):
+        for sub in range(2):
+            put(index, sub, partial(block, 0 if index == T2A else 1, sub))
+            parts[index, sub].start()
+            put(index2, sub, partial(block2, 1 if index2 == T2B else 0, sub))
+            parts[index2, sub].start()
+    at_a = [pl.ds(sub * quarter, quarter) for sub in range(2)]
+    at_b = [pl.ds(half + sub * quarter, quarter) for sub in range(2)]
+    for sub in range(2):
+        own[:, at_a[sub]] = partial(2, 0, sub)
+        own[:, at_b[sub]] = partial(1, 1, sub)
+    for sub in range(2):
+        parts[T2A, sub].wait_recv()
+        put(ACA, sub, own[:, at_a[sub]] + got(T2A, sub))
+        parts[ACA, sub].start()
+        parts[T2B, sub].wait_recv()
+        put(ACB, sub, own[:, at_b[sub]] + got(T2B, sub))
+        parts[ACB, sub].start()
     load_kin.wait()
-    for side in range(2):
-        at = pl.ds(side * half, half)
-        own[:, at] = partial(0, side) + kin_ref[:, at] * wbuf[pl.ds(0, rows), at].astype(
-            jnp.float32
-        )
-    la.wait_recv()
-    own[:, pl.ds(0, half)] += got(LA)
-    rb.wait_recv()
-    own[:, pl.ds(half, half)] += got(RB)
-    aca.wait_recv()
-    out_ref[:, pl.ds(0, half)] = (own[:, pl.ds(0, half)] + got(ACA)).astype(jnp.bfloat16)
-    acb.wait_recv()
-    out_ref[:, pl.ds(half, half)] = (own[:, pl.ds(half, half)] + got(ACB)).astype(jnp.bfloat16)
-
-    for c in (w0r, w1r, w1l, w0l, fr, fl, p0, p1, y_sum, to_twin, t2a, t2b, rb, la, aca, acb):
+    for side, at in enumerate((at_a, at_b)):
+        for sub in range(2):
+            own[:, at[sub]] = partial(0, side, sub) + kin_ref[:, at[sub]] * wbuf[
+                pl.ds(0, rows), at[sub]
+            ].astype(jnp.float32)
+    for sub in range(2):
+        parts[LA, sub].wait_recv()
+        own[:, at_a[sub]] += got(LA, sub)
+        parts[RB, sub].wait_recv()
+        own[:, at_b[sub]] += got(RB, sub)
+    for sub in range(2):
+        parts[ACA, sub].wait_recv()
+        out_ref[:, at_a[sub]] = (own[:, at_a[sub]] + got(ACA, sub)).astype(jnp.bfloat16)
+        parts[ACB, sub].wait_recv()
+        out_ref[:, at_b[sub]] = (own[:, at_b[sub]] + got(ACB, sub)).astype(jnp.bfloat16)
+
+    for c in (w0r, w1r, w1l, w0l, fr, fl, p0, p1, y_sum, to_twin, *parts.values()):
         c.wait_send()
     for c in (all_rs0, all_rs1, all_ag0, all_ag1):
         c.wait_send()
@@ -336,11 +351,11 @@
     bf16, f32 = jnp.bfloat16, jnp.float32
     share = 4 * rows // (2 * NZ)
     vmem = pl.BlockSpec(memory_space=pltpu.VMEM)
-    anywhere = pl.BlockSpec(memory_space=pl.ANY)
+    hbm = pl.BlockSpec(memory_space=pltpu.HBM)
     return pl.pallas_call(
         kernel,
         out_shape=jax.ShapeDtypeStruct((rows, cols), bf16),
-        in_specs=[anywhere, anywhere, anywhere, anywhere, vmem],
+        in_specs=[hbm, hbm, hbm, hbm, vmem],
         out_specs=vmem,
         scratch_shapes=[
             pltpu.VMEM((4 * rows, cols), bf16),

time: 93.4 us -> 92 us (0.985)
  Pallas kernels: 91.1 us -> 89.8 us
    pallas_call x1, Pallas kernels: 91.1 us -> 89.8 us  [local(): pl.pallas_call(kernel, out_shape=jax.ShapeDtypeStruct((rows, cols), bf16)...]
where the time goes in v3:
time: 92 us; the launch traced here: 91.9 us
  Pallas kernels  89.8 us (98%)
  local copies, waits for them, and re-layouts  2.06 us (2%)
    pallas_call x1, Pallas kernels, local(): pl.pallas_call(kernel, out_shape=jax.ShapeDtypeStruct((rows, cols), bf16)...  89.8 us
    unnamed x1, local copies, waits for them, and re-layouts  2.06 us

profile of v3, /device:TPU:1, one launch (start us, length us, event | category | flops | bytes accessed | tf_op | source)
XLA Modules:
  0.0 91.9 jit_solution(2417746592613107926)
XLA Ops:
  0.0 89.8 %shard_map.55 = bf16[128,3072]{1,0:T(8,128)(2,1)} custom-call(bf16[128,3072]{1,0:T(8,128)(2,1)} %w_hbm.1, bf16[256,3072]{1,0:T(8,128)(2,1)} %p_hbm.1, f32[1,3072]{1,0:T(1,128)} %bitcast.1, s32[256]{0:T(256)} %species_hbm.1, f32[4,8,8]{2,1,0:T(8,128)} %coupling_ref.1), custom_call_target="tpu_custom_call" | custom-call | tf_op jit(solution)/shard_map/pallas_call | solution.py:355
  89.8 2.1 %copy.7 = bf16[128,3072]{1,0:T(8,128)(2,1)} copy(bf16[128,3072]{1,0:T(8,128)(2,1)} %shard_map.55) | data formatting | bytes 1572864

commit v4 on v3

--- a/solution.py
+++ b/solution.py
@@ -93,22 +93,21 @@
         pl.semaphore_signal(barrier, inc=1, device_id=device, device_id_type=MESH)
     pl.semaphore_wait(barrier, len(near))
 
-    low, high = pl.ds(0, half_rows), pl.ds(half_rows, half_rows)
     wrow = lambda block, part: pl.ds(block * rows + part * half_rows, half_rows)
-    p0 = copy(P0, p_hbm.at[pl.ds(0, prows // 2)], pbuf.at[pl.ds(prows, prows // 2)], across)
-    p1 = copy(
-        P1,
-        p_hbm.at[pl.ds(prows // 2, prows // 2)],
-        pbuf.at[pl.ds(prows + prows // 2, prows // 2)],
-        across,
-    )
-    w0r = copy(W0R, w_hbm.at[low], wbuf.at[wrow(1, 0)], right)
-    w1r = copy(W1R, w_hbm.at[high], wbuf.at[wrow(1, 1)], right)
-    w1l = copy(W1L, w_hbm.at[high], wbuf.at[wrow(2, 1)], left)
-    w0l = copy(W0L, w_hbm.at[low], wbuf.at[wrow(2, 0)], left)
+    phalf = prows // 2
+    p0 = copy(P0, pbuf.at[pl.ds(0, phalf)], pbuf.at[pl.ds(prows, phalf)], across)
+    p1 = copy(P1, pbuf.at[pl.ds(phalf, phalf)], pbuf.at[pl.ds(prows + phalf, phalf)], across)
+    w0r = copy(W0R, wbuf.at[wrow(0, 0)], wbuf.at[wrow(1, 0)], right)
+    w1r = copy(W1R, wbuf.at[wrow(0, 1)], wbuf.at[wrow(1, 1)], right)
+    w1l = copy(W1L, wbuf.at[wrow(0, 1)], wbuf.at[wrow(2, 1)], left)
+    w0l = copy(W0L, wbuf.at[wrow(0, 0)], wbuf.at[wrow(2, 0)], left)
     fr = copy(FR, wbuf.at[wrow(1, 0)], wbuf.at[wrow(3, 0)], right)
     fl = copy(FL, wbuf.at[wrow(2, 1)], wbuf.at[wrow(3, 1)], left)
-    for c in (w0r, w1l, p0, w1r, w0l, p1):
+    load_p.wait()
+    p0.start()
+    p1.start()
+    load_w.wait()
+    for c in (w0r, w1l, w1r, w0l):
         c.start()
 
     load_species.wait()
@@ -175,18 +174,19 @@
     all_ag0 = many(AG0, dall.at[pl.ds(0, (npeers - 1) * piece), first])
     all_ag1 = many(AG1, dall.at[pl.ds(0, (nga - 1) * piece), last])
 
-    def scatter_first(low, count):
-        @pl.loop(0, count)
-        def _(k):
-            q = low + lax.rem(peer + k, count)
+    def scatter_first(row, count, at):
+        low, size = row // share, count // share
+
+        for k in range(size):
+            q = low + k
 
             @pl.when(q != peer)
             def _():
                 copy(
                     RS0,
-                    c0.at[pl.ds(pl.multiple_of(q * share, share), share)],
-                    r0.at[pl.ds(pl.multiple_of(peer * share, share), share)],
-                    at_place(lax.rem(q, NZ), y_hi, q // NZ),
+                    c0.at[pl.ds(q * share, share), at],
+                    r0.at[pl.ds(pl.multiple_of(peer * share, share), share), at],
+                    at_place(q % NZ, y_hi, q // NZ),
                 ).start()
 
     def other(k):
@@ -208,24 +208,31 @@
             preferred_element_type=jnp.float32,
         ).astype(jnp.bfloat16)
 
-    load_w.wait()
-    load_p.wait()
-    correlate(0, rows, 0, prows, c0, 0)
+    begun, added = pl.ds(0, prows), pl.ds(prows, phalf)
+
+    def correlate_first(row, count):
+        correlate(row, count, 0, prows, c0, 0)
+        scatter_first(row, count, begun)
+
+    correlate_first(0, rows)
     w0r.wait_recv()
     fr.start()
     w1l.wait_recv()
     fl.start()
+    correlate_first(rows, half_rows)
+    correlate_first(2 * rows + half_rows, half_rows)
+    p0.wait_recv()
+    correlate(0, rows, prows, phalf, c0, prows)
+    scatter_first(0, rows, added)
     w1r.wait_recv()
     w0l.wait_recv()
-    correlate(rows, 2 * rows, 0, prows, c0, 0)
-    p0.wait_recv()
-    correlate(0, 3 * rows, prows, prows // 2, c0, prows)
-    early = 3 * npeers // 4
-    scatter_first(0, early)
+    correlate_first(rows + half_rows, rows)
+    correlate(rows, 2 * rows, prows, phalf, c0, prows)
+    scatter_first(rows, 2 * rows, added)
     fr.wait_recv()
     fl.wait_recv()
-    correlate(3 * rows, rows, 0, prows + prows // 2, c0, 0)
-    scatter_first(early, npeers - early)
+    correlate(3 * rows, rows, 0, prows + phalf, c0, 0)
+    scatter_first(3 * rows, rows, first)
     here = pl.ds(pl.multiple_of(peer * share, share), share)
     r0[here, :] = c0[here, :]
 
@@ -237,25 +244,25 @@
     ysend[...] = sums[give, :].astype(jnp.bfloat16)
     y_sum = copy(RSY, ysend, yrecv, far)
     y_sum.start()
-    p1.wait_recv()
-    correlate(0, 4 * rows, prows + prows // 2, prows // 2, c1, 0)
-
-    @pl.loop(0, nga - 1)
-    def _(k):
-        at, device = other(k)
-        copy(RS1, c1.at[at], r1.at[mine], device).start()
-
-    r1[mine, :] = c1[mine, :]
-
     y_sum.wait_recv()
     for b in range(CUTS[0][1] // 128):
         at = pl.ds(b * 128, 128)
         dall[mine, at] = couple(sums[keep, at] + yrecv[:, at].astype(jnp.float32), b)
 
-    @pl.loop(0, npeers - 1)
+    @pl.loop(0, npeers - 1, unroll=True)
     def _(k):
         _, device = other(2 * k + 1)
         copy(AG0, dall.at[mine, first], dall.at[mine, first], device).start()
+
+    p1.wait_recv()
+    correlate(0, 4 * rows, prows + prows // 2, prows // 2, c1, 0)
+
+    @pl.loop(0, nga - 1, unroll=True)
+    def _(k):
+        at, device = other(k)
+        copy(RS1, c1.at[at], r1.at[mine], device).start()
+
+    r1[mine, :] = c1[mine, :]
 
     all_rs1.wait_recv()
     total = r1[pl.ds(0, piece), :].astype(jnp.float32)
@@ -263,7 +270,7 @@
         total += r1[pl.ds(q * piece, piece), :].astype(jnp.float32)
     dall[mine, last] = couple(total, 3)
 
-    @pl.loop(0, nga - 1)
+    @pl.loop(0, nga - 1, unroll=True)
     def _(k):
         _, device = other(k)
         copy(AG1, dall.at[mine, last], dall.at[mine, last], device).start()

time: 92 us -> 94 us (1.022)
  Pallas kernels: 89.8 us -> 91.7 us
    pallas_call x1, Pallas kernels: 89.8 us -> 91.7 us  [local(): pl.pallas_call(kernel, out_shape=jax.ShapeDtypeStruct((rows, cols), bf16)...]
where the time goes in v4:
time: 94 us; the launch traced here: 93.8 us
  Pallas kernels  91.7 us (98%)
  local copies, waits for them, and re-layouts  2.06 us (2%)
    pallas_call x1, Pallas kernels, local(): pl.pallas_call(kernel, out_shape=jax.ShapeDtypeStruct((rows, cols), bf16)...  91.7 us
    unnamed x1, local copies, waits for them, and re-layouts  2.06 us

profile of v4, /device:TPU:1, one launch (start us, length us, event | category | flops | bytes accessed | tf_op | source)
XLA Modules:
  0.0 93.8 jit_solution(11806277125127630300)
XLA Ops:
  0.0 91.7 %shard_map.55 = bf16[128,3072]{1,0:T(8,128)(2,1)} custom-call(bf16[128,3072]{1,0:T(8,128)(2,1)} %w_hbm.1, bf16[256,3072]{1,0:T(8,128)(2,1)} %p_hbm.1, f32[1,3072]{1,0:T(1,128)} %bitcast.1, s32[256]{0:T(256)} %species_hbm.1, f32[4,8,8]{2,1,0:T(8,128)} %coupling_ref.1), custom_call_target="tpu_custom_call" | custom-call | tf_op jit(solution)/shard_map/pallas_call | solution.py:362
  91.7 2.1 %copy.7 = bf16[128,3072]{1,0:T(8,128)(2,1)} copy(bf16[128,3072]{1,0:T(8,128)(2,1)} %shard_map.55) | data formatting | bytes 1572864
